TPU v7x, 128 devices: a whole 4x4x4 slice. The times are simulated.
128 devices in a mesh: expert: 32 (over z, y, x_hi), mp: 4 (over x_lo, core).
Axes of the slice: x: 4 (x_hi: 2, x_lo: 2; x = x_hi * 2 + x_lo), y: 4, z: 4, core: 2. Of those that a mesh axis runs over, the one named last changes fastest.
Arguments:
- queries: bfloat16 [1024, 48, 128], P('expert', 'mp'), may hold values from -140 to 140
- k_cache: bfloat16 [1024, 8, 128, 128], P('expert', 'mp'), may hold values from -5 to 5
- v_cache: bfloat16 [1024, 8, 128, 128], P('expert', 'mp'), may hold values from -6 to 6
- lengths: int32 [1024], P('expert'), may hold values from 2 to 128
- moe_input: bfloat16 [1024, 6144], P('expert', 'mp'), may hold values from -40 to 40
- norm_gain: float32 [6144], P('mp'), may hold values from 0.5 to 1.5
- expert_ids: int32 [1024, 2], P('expert'), may hold values from 0 to 7, all different within a row; in each aligned block of 32 rows (0 to 31, 32 to 63, ...) at most 16 rows name the same one
- combine_weights: float32 [1024, 2], P('expert'), may hold values from 0.1 to 1
- capacity: int32 [8], replicated, may hold values from 8 to 16
- w_gate: bfloat16 [32, 6144, 2048], P('expert', None, 'mp'), may hold values from -0.078125 to 0.078125
- w_up: bfloat16 [32, 6144, 2048], P('expert', None, 'mp'), may hold values from -0.078125 to 0.078125
- w_down: bfloat16 [32, 2048, 6144], P('expert', 'mp'), may hold values from -0.0625 to 0.0625
Outputs:
- context: bfloat16 [1024, 48, 128], P('expert', 'mp')
- layer_out: bfloat16 [1024, 6144], P('expert', 'mp')
Inputs may be any that keep to these rules, and one draw needn't show every extreme that they name: `expert_ids`: within each aligned block of 32 tokens, no expert is named by more than 16 tokens; the 2 ids of a token differ.
All inputs are finite; a program needn't handle non-finite values.
Results may differ from a plain program's by a relative error of at most 0.007.
Values may be sent and summed in bfloat16 or wider, within the bound.
A program may use at most 128 MiB of HBM per device.

v0:
```python
import jax
import jax.numpy as jnp
from jax import lax
from jax.sharding import PartitionSpec as P

D = 6144
EXPERTS = 8
TOP = 2


def copy_for_each(shard, axis):
    length = lax.axis_size(axis)
    return lax.all_to_all(
        jnp.broadcast_to(shard[None], (length, *shard.shape)), axis, 0, 0, tiled=True
    )


def taken_together(shard, axis):
    everything = copy_for_each(shard, axis)
    return jnp.sum(everything, axis=0)


def on_device(
    queries,
    k_cache,
    v_cache,
    lengths,
    moe_input,
    norm_gain,
    expert_ids,
    combine_weights,
    capacity,
    w_gate,
    w_up,
    w_down,
):
    seq_count, head_count, head_size = queries.shape
    kv_count = k_cache.shape[1]
    group_size = head_count // kv_count
    queries_grouped = queries.reshape(seq_count, kv_count, group_size, head_size)
    scores = jnp.einsum(
        "bjgd,bjpd->bjgp", queries_grouped, k_cache, preferred_element_type=jnp.float32
    ) * head_size ** (-0.5)
    positions = jnp.arange(k_cache.shape[2])
    live_mask = positions[None, :] < lengths[:, None]
    scores = jnp.where(live_mask[:, None, None, :], scores, -jnp.inf)
    top_score = jnp.max(scores, axis=-1, keepdims=True)
    expo = jnp.exp(scores - top_score)
    probs = (expo / jnp.sum(expo, axis=-1, keepdims=True)).astype(jnp.bfloat16)
    context = jnp.einsum("bjgp,bjpd->bjgd", probs, v_cache, preferred_element_type=jnp.float32)
    context = context.astype(jnp.bfloat16).reshape(seq_count, head_count, head_size)
    tok_rows, feat_width = moe_input.shape
    experts_total = lax.axis_size("expert")
    split_count = experts_total // EXPERTS
    slot_count = tok_rows // 2
    residual = moe_input.astype(jnp.float32)
    square_sum = taken_together(jnp.sum(residual * residual, axis=1), "mp")
    normed = (residual * lax.rsqrt(square_sum / D + 1e-05)[:, None] * norm_gain[None, :]).astype(
        jnp.bfloat16
    )
    flat_ids = expert_ids.reshape(-1)
    one_hot = (flat_ids[:, None] == jnp.arange(EXPERTS)[None, :]).astype(jnp.int32)
    earlier = jnp.cumsum(one_hot, axis=0) - one_hot
    slot_rank = jnp.sum(earlier * one_hot, axis=1)
    limits = jnp.sum(one_hot * capacity[None, :], axis=1)
    kept_mask = slot_rank < limits
    slot_id = flat_ids * slot_count + slot_rank
    select = (jnp.arange(EXPERTS * slot_count)[:, None] == slot_id[None, :]) & kept_mask[None, :]
    chosen = select.reshape(EXPERTS * slot_count, tok_rows, TOP).sum(axis=-1).astype(jnp.bfloat16)
    packed = jnp.dot(chosen, normed, preferred_element_type=jnp.float32).astype(jnp.bfloat16)
    packed_view = packed.reshape(EXPERTS, 1, slot_count, feat_width)
    outgoing = jnp.broadcast_to(
        packed_view, (EXPERTS, split_count, slot_count, feat_width)
    ).reshape(experts_total, slot_count, feat_width)
    arrived = lax.all_to_all(outgoing, "expert", split_axis=0, concat_axis=0, tiled=True)
    slot_rows = arrived.reshape(experts_total * slot_count, feat_width)
    gate_matrix = w_gate[0]
    up_matrix = w_up[0]
    piece = lax.all_gather(slot_rows, "mp", axis=1, tiled=True)
    gate_sum = jnp.dot(piece, gate_matrix, preferred_element_type=jnp.float32)
    up_sum = jnp.dot(piece, up_matrix, preferred_element_type=jnp.float32)
    hidden = (jax.nn.silu(gate_sum) * up_sum).astype(jnp.bfloat16)
    down_terms = jnp.dot(hidden, w_down[0], preferred_element_type=jnp.float32)
    result = lax.psum_scatter(
        down_terms.astype(jnp.bfloat16), "mp", scatter_dimension=1, tiled=True
    ).astype(jnp.float32)
    result = result.reshape(experts_total, slot_count, feat_width)
    returned = lax.all_to_all(
        result.astype(jnp.bfloat16), "expert", split_axis=0, concat_axis=0, tiled=True
    ).astype(result.dtype)
    gathered = returned.reshape(EXPERTS, split_count, slot_count, feat_width).sum(axis=1)
    weighted = select.astype(jnp.float32) * combine_weights.reshape(-1)[None, :]
    weighted = weighted.reshape(EXPERTS * slot_count, tok_rows, TOP).sum(axis=-1)
    added = jnp.dot(
        weighted.T,
        gathered.reshape(EXPERTS * slot_count, feat_width),
        precision=lax.Precision.HIGHEST,
        preferred_element_type=jnp.float32,
    )
    layer_out = (residual + added).astype(jnp.bfloat16)
    return (context, layer_out)


def solution(mesh):
    in_specs = (
        P("expert", "mp", None),
        P("expert", "mp", None, None),
        P("expert", "mp", None, None),
        P("expert"),
        P("expert", "mp"),
        P("mp"),
        P("expert", None),
        P("expert", None),
        P(),
        P("expert", None, "mp"),
        P("expert", None, "mp"),
        P("expert", "mp", None),
    )
    out_specs = (P("expert", "mp", None), P("expert", "mp"))
    return jax.shard_map(
        on_device, mesh=mesh, in_specs=in_specs, out_specs=out_specs, check_vma=False
    )
```

profile of v0, /device:TPU:0, one launch (start us, length us, event | category | flops | bytes accessed | tf_op | source)
XLA Modules:
  0.0 241.0 jit_solution(17255489095388634369)
XLA Ops:
  7.2 0.0 copy-start
  7.2 1.2 fusion.16
  8.3 0.6 broadcast_in_dim.20
  8.9 3.2 %all-to-all-start = ((f32[4,1,32]{2,1,0:T(1,128)}), f32[4,1,32]{2,1,0:T(1,128)S(1)}, u32[]{:S(2)}, u32[]{:S(2)}) async-start(f32[4,1,32]{2,1,0:T(1,128)} %broadcast_in_dim.20), calls=%async_computation | async-start | bytes 4096 | tf_op jit(solution)/shard_map/all_to_all | solution.py:13
  12.2 0.0 all-gather.2.cloned.1.call-start
  12.2 0.8 copy.43
  13.0 0.1 eq.31
  13.1 0.1 fusion.24
  13.2 0.1 reduce_window_sum.11
  13.3 0.8 select_reduce_fusion.1
  14.1 0.1 reduce_sum.78
  14.2 0.1 reduce_sum.80
  14.3 0.1 copy.44
  14.4 0.1 copy.45
  14.5 0.7 multiply_add_fusion
  15.2 0.1 convert_reduce_fusion.1
  15.3 0.5 all-to-all-done
  15.9 1.2 convolution_convert_fusion.1
  17.1 0.2 broadcast_in_dim.22
  17.3 35.8 %all_to_all.16 = bf16[32,16,1536]{2,1,0:T(8,128)(2,1)} all-to-all(bf16[32,16,1536]{2,1,0:T(8,128)(2,1)S(1)} %bitcast.34), channel_id=1, replica_groups=mesh['expert'=32,'mp'=4] {'expert'}, dimensions={0} | all-to-all | bytes 3145728 | tf_op jit(solution)/shard_map/all_to_all | solution.py:75
  53.1 0.0 all-gather.2.cloned.1.call-update
  53.1 0.0 reduce-scatter.2.cloned.1.call-start
  53.1 58.8 %all-gather.2.cloned.1.call-done = bf16[512,6144]{1,0:T(8,128)(2,1)} async-done(((bf16[512,1536]{1,0:T(8,128)(2,1)}), bf16[512,6144]{1,0:T(8,128)(2,1)}) %all-gather.2.cloned.1.call-update) | async-done | bytes 6291472 | tf_op jit(solution)/shard_map/all_gather | solution.py:79
  111.9 8.2 %fusion.4 = f32[512,512]{1,0:T(8,128)S(1)} fusion(bf16[512,6144]{1,0:T(8,128)(2,1)} %all-gather.2.cloned.1.call-done, bf16[1,6144,512]{2,1,0:T(8,128)(2,1)} %param.21), kind=kOutput, calls=%fused_computation.5 | convolution fusion | flops 3221225472 | bytes 13631488 | tf_op jit(solution)/shard_map/dot_general | solution.py:80
  120.1 0.0 copy-done.5
  120.1 0.0 slice-start.1
  120.2 6.4 %fusion.10 = bf16[512,512]{1,0:T(8,128)(2,1)S(1)} fusion(bf16[512,6144]{1,0:T(8,128)(2,1)S(1)} %copy-done.5, bf16[1,6144,512]{2,1,0:T(8,128)(2,1)} %param.22, f32[512,512]{1,0:T(8,128)S(1)} %fusion.4), kind=kOutput, calls=%fused_computation.12 | convolution fusion | flops 3222798336 | bytes 14155776 | tf_op jit(solution)/shard_map/dot_general | solution.py:81
  126.6 0.0 slice-done
  126.6 0.0 slice-done.1
  126.6 5.3 %convolution_convert_fusion = bf16[512,6144]{1,0:T(8,128)(2,1)} fusion(bf16[512,512]{1,0:T(8,128)(2,1)S(1)} %fusion.10, bf16[1,512,6144]{2,1,0:T(8,128)(2,1)S(1)} %bitcast.42), kind=kOutput, calls=%fused_computation.1 | convolution fusion | flops 3224371200 | bytes 13107200 | tf_op jit(solution)/shard_map/dot_general | solution.py:83
  132.0 0.0 reduce-scatter.2.cloned.1.call-update
  132.0 0.0 copy-start.1
  132.0 64.4 %reduce-scatter.2.cloned.1.call-done = bf16[512,1536]{1,0:T(8,128)(2,1)} async-done(((bf16[512,6144]{1,0:T(8,128)(2,1)}), bf16[512,1536]{1,0:T(8,128)(2,1)}) %reduce-scatter.2.cloned.1.call-update) | async-done | bytes 1572880 | tf_op jit(solution)/shard_map/reduce_scatter | solution.py:84
  196.5 9.5 %all-to-all-start.2 = ((bf16[32,16,1536]{2,1,0:T(8,128)(2,1)}), bf16[32,16,1536]{2,1,0:T(8,128)(2,1)}, u32[]{:S(2)}, u32[]{:S(2)}) async-start(bf16[32,16,1536]{2,1,0:T(8,128)(2,1)} %bitcast.36), calls=%async_computation.3 | async-start | bytes 3145728 | tf_op jit(solution)/shard_map/all_to_all | solution.py:88
  206.0 0.0 copy-done.4
  206.0 0.1 iota_compare_fusion.2
  206.0 0.0 copy-done
  206.0 0.0 copy-done.2
  206.0 1.2 fusion.14
  207.2 0.3 fusion.27
  207.5 2.5 %convolution_convert_fusion.2 = bf16[32,2,6,128]{3,2,1,0:T(8,128)(2,1)S(1)} fusion(bf16[32,2,128,128]{3,2,1,0:T(8,128)(2,1)} %param.14, f32[32,2,6]{2,1,0:T(2,128)S(1)} %fusion.27, f32[32,2,6,128]{3,2,1,0:T(8,128)S(1)} %fusion.14), kind=kOutput, calls=%fused_computation.17 | convolution fusion | flops 12780031 | bytes 2393600 | tf_op jit(solution)/shard_map/bjgp,bjpd->bjgd/dot_general | solution.py:50
  210.0 0.7 copy.42
  210.7 0.0 copy-done.3
  210.7 0.1 select_reduce_fusion
  210.8 20.4 %all-to-all-done.2 = bf16[32,16,1536]{2,1,0:T(8,128)(2,1)} async-done(((bf16[32,16,1536]{2,1,0:T(8,128)(2,1)}), bf16[32,16,1536]{2,1,0:T(8,128)(2,1)}, u32[]{:S(2)}, u32[]{:S(2)}) %all-to-all-start.2) | async-done | bytes 1572896 | tf_op jit(solution)/shard_map/all_to_all | solution.py:88
  231.2 1.8 convert_reduce_fusion
  233.0 0.0 copy-done.1
  233.0 1.2 fusion.6
  (9 shorter events, 0.0 us)
Async XLA Ops:
  7.2 198.9 %copy-start = (bf16[32,2,128,128]{3,2,1,0:T(8,128)(2,1)S(1)}, bf16[32,2,128,128]{3,2,1,0:T(8,128)(2,1)}, u32[]{:S(2)}) copy-start(bf16[32,2,128,128]{3,2,1,0:T(8,128)(2,1)} %param.13) | copy-start | bytes 6291460
  8.9 6.9 %all-to-all-start = ((f32[4,1,32]{2,1,0:T(1,128)}), f32[4,1,32]{2,1,0:T(1,128)S(1)}, u32[]{:S(2)}, u32[]{:S(2)}) async-start(f32[4,1,32]{2,1,0:T(1,128)} %broadcast_in_dim.20), calls=%async_computation | async-start | bytes 4096 | tf_op jit(solution)/shard_map/all_to_all | solution.py:13
  12.2 99.8 %all-gather.2.cloned.1.call-start = ((), (), s32[]{:S(2)}) async-start(), calls=%async_computation.4 | async-start | bytes 7864320 | tf_op jit(solution)/shard_map/all_gather | solution.py:79
  53.1 143.4 %reduce-scatter.2.cloned.1.call-start = ((), (), s32[]{:S(2)}) async-start(), calls=%async_computation.5 | async-start | bytes 7864320 | tf_op jit(solution)/shard_map/reduce_scatter | solution.py:84
  111.9 8.2 %copy-start.5 = (bf16[512,6144]{1,0:T(8,128)(2,1)S(1)}, bf16[512,6144]{1,0:T(8,128)(2,1)}, u32[]{:S(2)}) copy-start(bf16[512,6144]{1,0:T(8,128)(2,1)} %all-gather.2.cloned.1.call-done) | copy-start | bytes 18874372
  111.9 14.7 %slice-start = ((s8[6291456]{0:T(1024)(128)(4,1)}), s8[4194304]{0:T(1024)(128)(4,1)S(1)}, s32[]{:S(2)}) async-start(s8[6291456]{0:T(1024)(128)(4,1)} %bitcast.41), calls=%async_computation.6 | async-start | bytes 8388608
  120.1 6.5 %slice-start.1 = ((s8[6291456]{0:T(1024)(128)(4,1)}), s8[2097152]{0:T(1024)(128)(4,1)S(1)}, s32[]{:S(2)}) async-start(s8[6291456]{0:T(1024)(128)(4,1)} %bitcast.41), calls=%async_computation.7 | async-start | bytes 4194304
  132.0 74.0 %copy-start.4 = (s32[32]{0:T(128)S(1)}, s32[32]{0:T(128)}, u32[]{:S(2)}) copy-start(s32[32]{0:T(128)} %param.15) | copy-start | bytes 388
  132.0 74.1 %copy-start.2 = (bf16[32,12,128]{2,0,1:T(8,128)(2,1)S(1)}, bf16[32,12,128]{2,0,1:T(8,128)(2,1)}, u32[]{:S(2)}) copy-start(bf16[32,12,128]{2,0,1:T(8,128)(2,1)} %param.12) | copy-start | bytes 294916
  132.0 78.7 %copy-start.3 = (f32[32,2]{0,1:T(2,128)S(1)}, f32[32,2]{0,1:T(2,128)}, u32[]{:S(2)}) copy-start(f32[32,2]{0,1:T(2,128)} %param.19) | copy-start | bytes 772
  132.0 101.0 %copy-start.1 = (bf16[32,1536]{1,0:T(8,128)(2,1)S(1)}, bf16[32,1536]{1,0:T(8,128)(2,1)}, u32[]{:S(2)}) copy-start(bf16[32,1536]{1,0:T(8,128)(2,1)} %param.16) | copy-start | bytes 294916
  196.5 34.8 %all-to-all-start.2 = ((bf16[32,16,1536]{2,1,0:T(8,128)(2,1)}), bf16[32,16,1536]{2,1,0:T(8,128)(2,1)}, u32[]{:S(2)}, u32[]{:S(2)}) async-start(bf16[32,16,1536]{2,1,0:T(8,128)(2,1)} %bitcast.36), calls=%async_computation.3 | async-start | bytes 3145728 | tf_op jit(solution)/shard_map/all_to_all | solution.py:88
Sparse Core Ops, SparseCore 0:
  53.2 58.6 all-gather.1
  132.1 64.2 reduce-scatter.1
where the time goes:
time: 241 us
  waiting for transfers between devices  144 us (60%)
  blocking collectives  35.8 us (15%)
  matrix products  26 us (11%)
  between operations  14.2 us (6%)
  starting transfers between devices  12.8 us (5%)
  other arithmetic  5.19 us (2%)
  local copies, waits for them, and re-layouts  2.72 us (1%)
    reduce_scatter x1, waiting for transfers between devices, on_device(): lax.psum_scatter(down_terms.astype(jnp.bfloat16), 'mp', scatter_dimension...  64.4 us
    all_gather x1, waiting for transfers between devices, on_device(): piece = lax.all_gather(slot_rows, 'mp', axis=1, tiled=True)  58.8 us
    all_to_all x1, blocking collectives, on_device(): lax.all_to_all(outgoing, 'expert', split_axis=0, concat_axis=0, tiled=True)  35.8 us
    all_to_all x1, waiting for transfers between devices, on_device(): lax.all_to_all(result.astype(jnp.bfloat16), 'expert', split_axis=0, conca...  20.4 us
    all_to_all x1, starting transfers between devices, on_device(): lax.all_to_all(result.astype(jnp.bfloat16), 'expert', split_axis=0, conca...  9.5 us
    dot_general x1, matrix products, on_device(): gate_sum = jnp.dot(piece, gate_matrix, preferred_element_type=jnp.float32)  8.19 us
    dot_general x1, matrix products, on_device(): up_sum = jnp.dot(piece, up_matrix, preferred_element_type=jnp.float32)  6.43 us
    dot_general x1, matrix products, on_device(): down_terms = jnp.dot(hidden, w_down[0], preferred_element_type=jnp.float32)  5.35 us
  transfers between devices with their start and end apart: 4, of which 4 were waited for; matrix products, arithmetic and copies ran while one was open for 3% of the time, Pallas kernels for 0%

commit v1 on v0

v1 whole, which is shorter than its diff:
```python
import jax
import jax.numpy as jnp
from jax import lax
from jax.experimental import pallas as pl
from jax.experimental.pallas import tpu as pltpu
from jax.sharding import PartitionSpec as P

MESH = pl.DeviceIdType.MESH
F32 = jnp.float32
BF16 = jnp.bfloat16

D = 6144
EXPERTS = 8
SLOTS = 16
TOK = 32
FEAT = 1536
HID = 512
ROWS = 512
SEQS = 32
STEP = (0, 1, 3, 2)


def base(h, p):
    return (p // 2) * 256 + h * 128 + (p % 2) * 64


def kernel(
    lengths,
    capacity,
    q_ref,
    x_ref,
    gain_ref,
    ids_ref,
    wts_ref,
    k_hbm,
    v_hbm,
    wg_hbm,
    wu_hbm,
    wd_hbm,
    ctx_ref,
    out_ref,
    kv,
    vv,
    wg,
    wu,
    wd,
    xb,
    pk,
    acc_g,
    acc_u,
    hid,
    ps,
    pr,
    q1,
    q0,
    xr,
    own,
    rb,
    sq,
    rt,
    nm,
    fin,
    w_sem,
    kv_sem,
    sq_s,
    sq_r,
    rt_s,
    rt_r,
    nm_s,
    nm_r,
    s1_s,
    s1_r,
    xf_s,
    xf_r,
    dd_s,
    dd_r,
    pr_s,
    pr_r,
    xq_s,
    xq_r,
    r2_s,
    r2_r,
    fin_s,
    fin_r,
):
    s = lax.axis_index("expert")
    m = lax.axis_index("mp")
    z = s // 8
    y = (s // 2) % 4
    s_other = s + 1 - 2 * (s % 2)
    m_core = m + 1 - 2 * (m % 2)
    m_near = (m + 2) % 4
    m_both = 3 - m
    mates = (m, m_core, m_near, m_both)
    x_hi = s % 2
    mate = (s, m_core)
    near = (s, m_near)
    far = (s_other, m_near)
    opp = (s_other, m)

    def plane(dz, dy):
        return (((z + dz) % 4) * 8 + ((y + dy) % 4) * 2 + x_hi, m)

    def send(src, dst, send_sem, recv_sem, device):
        pltpu.make_async_remote_copy(
            src_ref=src,
            dst_ref=dst,
            send_sem=send_sem,
            recv_sem=recv_sem,
            device_id=device,
            device_id_type=MESH,
        ).start()

    def wait(ref, sem):
        pltpu.make_async_copy(ref, ref, sem).wait()

    copies = []
    for k in range(4):
        rows = pl.ds(pl.multiple_of(mates[k] * FEAT, FEAT), FEAT)
        copies.append(pltpu.make_async_copy(wg_hbm.at[0, rows, :], wg.at[k], w_sem.at[0, k]))
        copies.append(pltpu.make_async_copy(wu_hbm.at[0, rows, :], wu.at[k], w_sem.at[1, k]))
        copies.append(pltpu.make_async_copy(wd_hbm.at[0, :, rows], wd.at[k], w_sem.at[2, k]))
    k_copy = pltpu.make_async_copy(k_hbm, kv, kv_sem.at[0])
    v_copy = pltpu.make_async_copy(v_hbm, vv, kv_sem.at[1])
    k_copy.start()
    v_copy.start()
    for copy in copies:
        copy.start()

    barrier = pltpu.get_barrier_semaphore()
    partners = [plane(dz, dy) for dz in range(4) for dy in range(4) if (dz, dy) != (0, 0)]
    partners += [mate, near, far, opp, (s, m_both)]
    for device in partners:
        pl.semaphore_signal(barrier, inc=1, device_id=device, device_id_type=MESH)

    lane = lax.broadcasted_iota(jnp.int32, (TOK, 128), 1)
    ids = ids_ref[...].astype(F32)
    wts = wts_ref[...]
    route = jnp.where(
        lane == 0,
        ids[:, 0:1],
        jnp.where(lane == 1, ids[:, 1:2], jnp.where(lane == 2, wts[:, 0:1], wts[:, 1:2])),
    )
    rt[0] = route
    x = x_ref[...].astype(F32)
    mine = jnp.sum(x * x, axis=1, keepdims=True)
    sq[0] = jnp.broadcast_to(mine, (TOK, 128))

    pl.semaphore_wait(barrier, len(partners))
    for k in range(1, 4):
        send(sq.at[0], sq.at[k], sq_s, sq_r.at[k], (s, mates[k]))
    send(rt.at[0], rt.at[1], rt_s, rt_r, opp)

    col = lax.broadcasted_iota(jnp.int32, (TOK, 256), 1)
    group = col // 64
    dz_col = jnp.where(group == 3, 2, jnp.where(group == 2, 3, group))
    e_col = ((z + dz_col) % 4) * 2 + ((y + (col // 16) % 4) % 4) // 2
    j_col = col % 16
    cap_col = jnp.zeros((TOK, 256), jnp.int32)
    for e in range(EXPERTS):
        cap_col = jnp.where(e_col == e, capacity[e], cap_col)
    open_col = j_col < cap_col
    e_col_f = e_col.astype(F32)
    j_col_f = j_col.astype(F32)
    tri = (
        lax.broadcasted_iota(jnp.int32, (TOK, TOK), 1)
        < lax.broadcasted_iota(jnp.int32, (TOK, TOK), 0)
    ).astype(F32).astype(BF16)

    def routing(route):
        first = route[:, 0:1] == e_col_f
        second = route[:, 1:2] == e_col_f
        member = first | second
        rank = jnp.dot(tri, member.astype(F32).astype(BF16), preferred_element_type=F32)
        take = member & (rank == j_col_f) & open_col
        weight = jnp.where(take, jnp.where(first, route[:, 2:3], route[:, 3:4]), 0.0)
        return take.astype(F32).astype(BF16), weight

    take_own, weight_own = routing(route)

    for k in range(1, 4):
        wait(sq.at[k], sq_r.at[k])
    total = (sq[0] + sq[1] + sq[2] + sq[3])[:, 0:1]
    normed = (x * lax.rsqrt(total / D + 1e-05) * gain_ref[...]).astype(BF16)
    nm[0] = normed
    send(nm.at[0], nm.at[1], nm_s, nm_r, opp)

    def pack(h, take, features):
        packed = lax.dot_general(
            take, features, (((0,), (0,)), ((), ())), preferred_element_type=F32
        ).astype(BF16)
        pk[h] = packed
        xb[0, 0, base(h, 0) : base(h, 0) + SLOTS, :] = packed[0:SLOTS, :]
        for p in range(4):
            for dy in range(4):
                if p == 0 and dy == 0:
                    continue
                at = base(h, p) + dy * SLOTS
                send(
                    pk.at[h, pl.ds(p * 64 + dy * SLOTS, SLOTS), :],
                    xb.at[0, 0, pl.ds(at, SLOTS), :],
                    s1_s.at[h],
                    s1_r.at[h, p],
                    plane(STEP[p], dy),
                )

    def wait_slots(h, p):
        if p == 0:
            wait(xb.at[0, 0, pl.ds(base(h, p) + SLOTS, 48), :], s1_r.at[h, p])
        else:
            wait(xb.at[0, 0, pl.ds(base(h, p), 64), :], s1_r.at[h, p])

    def to_mate(kx, h, p):
        rows = pl.ds(base(h, p), 64)
        send(xb.at[kx, 0, rows, :], xb.at[kx, 1, rows, :], dd_s.at[kx], dd_r.at[kx, p // 2], mate)

    def forward_own(p):
        wait_slots(0, p)
        rows = pl.ds(base(0, p), 64)
        send(xb.at[0, 0, rows, :], xb.at[1, 0, rows, :], xf_s.at[0], xf_r.at[0, p], near)
        send(
            xb.at[0, 0, rows, :],
            xb.at[1, 0, pl.ds(base(1, p), 64), :],
            xf_s.at[1],
            xf_r.at[1, p],
            far,
        )
        to_mate(0, 0, p)

    def forward_opp(p):
        wait_slots(1, p)
        to_mate(0, 1, p)

    def forward_side(p):
        for h in range(2):
            wait(xb.at[1, 0, pl.ds(base(h, p), 64), :], xf_r.at[h, p])
            to_mate(1, h, p)

    position = lax.broadcasted_iota(jnp.int32, (12, 256), 1)
    head = lax.broadcasted_iota(jnp.int32, (12, 128), 0)
    low_head = head < 6
    position = position[:, 0:128]

    def attend(b):
        scores = lax.dot_general(
            q_ref[b],
            kv[b].reshape(256, 128),
            (((1,), (1,)), ((), ())),
            preferred_element_type=F32,
        )
        scores = jnp.where(low_head, scores[:, 0:128], scores[:, 128:256]) * 128 ** (-0.5)
        scores = jnp.where(position < lengths[b], scores, -jnp.inf)
        expo = jnp.exp(scores - jnp.max(scores, axis=1, keepdims=True))
        probs = expo / jnp.sum(expo, axis=1, keepdims=True)
        both = jnp.concatenate(
            [jnp.where(low_head, probs, 0.0), jnp.where(low_head, 0.0, probs)], axis=1
        ).astype(BF16)
        ctx_ref[b] = jnp.dot(
            both, vv[b].reshape(256, 128), preferred_element_type=F32
        ).astype(BF16)

    def attention(first, count):
        def some(i, carry):
            for u in range(8):
                attend(first + i * 8 + u)
            return carry

        lax.fori_loop(0, count // 8, some, 0)

    pack(0, take_own, normed)
    k_copy.wait()
    v_copy.wait()
    attention(0, 8)
    wait(rt.at[1], rt_r)
    take_opp, weight_opp = routing(rt[1])
    forward_own(0)
    wait(nm.at[1], nm_r)
    pack(1, take_opp, nm[1])
    forward_own(1)
    attention(8, 8)
    forward_own(2)
    forward_opp(0)
    attention(16, 8)
    forward_own(3)
    forward_opp(1)
    forward_side(0)
    attention(24, 8)

    def gate_up(k, half):
        kx, cc = k // 2, k % 2
        rows = pl.ds(half * 256, 256)
        for n in range(2):
            cols = pl.ds(n * 256, 256)
            g = jnp.dot(xb[kx, cc, rows, :], wg[k, :, cols], preferred_element_type=F32)
            u = jnp.dot(xb[kx, cc, rows, :], wu[k, :, cols], preferred_element_type=F32)
            if k != 0:
                g = g + acc_g[rows, cols]
                u = u + acc_u[rows, cols]
            if k != 3:
                acc_g[rows, cols] = g
                acc_u[rows, cols] = u
            else:
                hid[rows, cols] = (g / (1.0 + jnp.exp(-g)) * u).astype(BF16)

    def weights(kind, k):
        copies[k * 3 + kind].wait()

    weights(0, 0)
    weights(1, 0)
    gate_up(0, 0)
    forward_opp(2)
    forward_side(1)
    weights(0, 1)
    weights(1, 1)
    wait(xb.at[0, 1, pl.ds(0, 256), :], dd_r.at[0, 0])
    gate_up(1, 0)
    forward_opp(3)
    gate_up(0, 1)
    weights(0, 2)
    weights(1, 2)
    gate_up(2, 0)
    forward_side(2)
    wait(xb.at[0, 1, pl.ds(256, 256), :], dd_r.at[0, 1])
    gate_up(1, 1)
    weights(0, 3)
    weights(1, 3)
    wait(xb.at[1, 1, pl.ds(0, 256), :], dd_r.at[1, 0])
    gate_up(3, 0)
    forward_side(3)
    gate_up(2, 1)
    wait(xb.at[1, 1, pl.ds(256, 256), :], dd_r.at[1, 1])
    gate_up(3, 1)

    def down(k, half, n):
        return jnp.dot(
            hid[half * 256 : half * 256 + 256, :],
            wd[k, :, n * 512 : n * 512 + 512],
            preferred_element_type=F32,
        )

    def down_for_mate(kx, half):
        for n in range(3):
            ps[kx, half, :, n * 512 : n * 512 + 512] = down(kx * 2 + 1, half, n).astype(BF16)
        send(ps.at[kx, half], pr.at[kx, half], pr_s.at[kx, half], pr_r.at[kx, half], mate)

    def down_mine(kx, half, dst):
        wait(pr.at[kx, half], pr_r.at[kx, half])
        for n in range(3):
            cols = slice(n * 512, n * 512 + 512)
            terms = down(kx * 2, half, n) + pr[kx, half, :, cols].astype(F32)
            dst[half * 256 : half * 256 + 256, cols] = terms.astype(BF16)

    def to_sides(p):
        for h, device in ((0, near), (1, far)):
            send(
                q1.at[pl.ds(base(h, p), 64), :],
                xr.at[h, pl.ds(p * 64, 64), :],
                xq_s.at[h],
                xq_r.at[h, p],
                device,
            )

    def home(h, p, src, first):
        for dy in range(4):
            at = pl.ds(p * 64 + dy * SLOTS, SLOTS)
            if p == 0 and dy == 0:
                rb[h, 0:SLOTS, :] = src[first : first + SLOTS, :]
                continue
            send(
                src.at[pl.ds(first + dy * SLOTS, SLOTS), :],
                rb.at[h, at, :],
                r2_s.at[h],
                r2_r.at[h, p],
                plane(-STEP[p] + 4, -dy + 4),
            )

    def wait_home(h):
        wait(rb.at[h, pl.ds(SLOTS, 48), :], r2_r.at[h, 0])
        for p in range(1, 4):
            wait(rb.at[h, pl.ds(p * 64, 64), :], r2_r.at[h, p])

    def combine(h, weight):
        high = weight.astype(BF16)
        rest = weight - high.astype(F32)
        middle = rest.astype(BF16)
        low = (rest - middle.astype(F32)).astype(BF16)
        stacked = jnp.concatenate([high, middle, low], axis=0)
        terms = jnp.dot(stacked, rb[h], preferred_element_type=F32)
        return terms[0:TOK] + terms[TOK : 2 * TOK] + terms[2 * TOK : 3 * TOK]

    weights(2, 3)
    down_for_mate(1, 1)
    down_for_mate(1, 0)
    weights(2, 2)
    down_mine(1, 1, q1)
    to_sides(3)
    to_sides(2)
    down_mine(1, 0, q1)
    to_sides(1)
    to_sides(0)
    weights(2, 1)
    down_for_mate(0, 1)
    down_for_mate(0, 0)
    weights(2, 0)
    down_mine(0, 1, q0)
    home(1, 3, q0, base(1, 3))
    home(1, 2, q0, base(1, 2))
    down_mine(0, 0, q0)
    home(1, 1, q0, base(1, 1))
    home(1, 0, q0, base(1, 0))

    for p in (3, 2, 1, 0):
        rows = slice(p * 64, p * 64 + 64)
        for h in range(2):
            wait(xr.at[h, pl.ds(p * 64, 64), :], xq_r.at[h, p])
        terms = q0[base(0, p) : base(0, p) + 64, :].astype(F32)
        terms = terms + xr[0, rows, :].astype(F32) + xr[1, rows, :].astype(F32)
        own[rows, :] = terms.astype(BF16)
        home(0, p, own, p * 64)
        if p == 1:
            wait_home(1)
            fin[0] = combine(1, weight_opp).astype(BF16)
            send(fin.at[0], fin.at[1], fin_s, fin_r, opp)

    wait_home(0)
    added = combine(0, weight_own)
    wait(fin.at[1], fin_r)
    out_ref[...] = (x_ref[...].astype(F32) + (added + fin[1].astype(F32))).astype(BF16)

    wait(sq.at[pl.ds(0, 3)], sq_s)
    wait(rt.at[0], rt_s)
    wait(nm.at[0], nm_s)
    for h in range(2):
        wait(pk.at[h, pl.ds(SLOTS, 240), :], s1_s.at[h])
        wait(xb.at[0, 0, pl.ds(0, 256), :], xf_s.at[h])
        wait(xb.at[h, 0], dd_s.at[h])
        for half in range(2):
            wait(ps.at[h, half], pr_s.at[h, half])
        wait(xr.at[h], xq_s.at[h])
        wait(rb.at[h, pl.ds(SLOTS, 240), :], r2_s.at[h])
    wait(fin.at[0], fin_s)


def on_device(
    queries,
    k_cache,
    v_cache,
    lengths,
    moe_input,
    norm_gain,
    expert_ids,
    combine_weights,
    capacity,
    w_gate,
    w_up,
    w_down,
):
    vmem = pl.BlockSpec(memory_space=pltpu.VMEM)
    smem = pl.BlockSpec(memory_space=pltpu.SMEM)
    hbm = pl.BlockSpec(memory_space=pl.ANY)
    dma = pltpu.SemaphoreType.DMA
    return pl.pallas_call(
        kernel,
        out_shape=(
            jax.ShapeDtypeStruct(queries.shape, BF16),
            jax.ShapeDtypeStruct(moe_input.shape, BF16),
        ),
        in_specs=[smem, smem, vmem, vmem, vmem, vmem, vmem, hbm, hbm, hbm, hbm, hbm],
        out_specs=(vmem, vmem),
        scratch_shapes=[
            pltpu.VMEM((SEQS, 2, 128, 128), BF16),
            pltpu.VMEM((SEQS, 2, 128, 128), BF16),
            pltpu.VMEM((4, FEAT, HID), BF16),
            pltpu.VMEM((4, FEAT, HID), BF16),
            pltpu.VMEM((4, HID, FEAT), BF16),
            pltpu.VMEM((2, 2, ROWS, FEAT), BF16),
            pltpu.VMEM((2, 256, FEAT), BF16),
            pltpu.VMEM((ROWS, HID), F32),
            pltpu.VMEM((ROWS, HID), F32),
            pltpu.VMEM((ROWS, HID), BF16),
            pltpu.VMEM((2, 2, 256, FEAT), BF16),
            pltpu.VMEM((2, 2, 256, FEAT), BF16),
            pltpu.VMEM((ROWS, FEAT), BF16),
            pltpu.VMEM((ROWS, FEAT), BF16),
            pltpu.VMEM((2, 256, FEAT), BF16),
            pltpu.VMEM((256, FEAT), BF16),
            pltpu.VMEM((2, 256, FEAT), BF16),
            pltpu.VMEM((4, TOK, 128), F32),
            pltpu.VMEM((2, TOK, 128), F32),
            pltpu.VMEM((2, TOK, FEAT), BF16),
            pltpu.VMEM((2, TOK, FEAT), BF16),
            dma((3, 4)),
            dma((2,)),
            dma,
            dma((4,)),
            dma,
            dma,
            dma,
            dma,
            dma((2,)),
            dma((2, 4)),
            dma((2,)),
            dma((2, 4)),
            dma((2,)),
            dma((2, 2)),
            dma((2, 2)),
            dma((2, 2)),
            dma((2,)),
            dma((2, 4)),
            dma((2,)),
            dma((2, 4)),
            dma,
            dma,
        ],
        compiler_params=pltpu.CompilerParams(
            collective_id=0, has_side_effects=True, vmem_limit_bytes=62 * 1024 * 1024
        ),
    )(
        lengths,
        capacity,
        queries,
        moe_input,
        norm_gain.reshape(1, FEAT),
        expert_ids,
        combine_weights,
        k_cache,
        v_cache,
        w_gate,
        w_up,
        w_down,
    )


def solution(mesh):
    in_specs = (
        P("expert", "mp", None),
        P("expert", "mp", None, None),
        P("expert", "mp", None, None),
        P("expert"),
        P("expert", "mp"),
        P("mp"),
        P("expert", None),
        P("expert", None),
        P(),
        P("expert", None, "mp"),
        P("expert", None, "mp"),
        P("expert", "mp", None),
    )
    out_specs = (P("expert", "mp", None), P("expert", "mp"))
    return jax.shard_map(
        on_device, mesh=mesh, in_specs=in_specs, out_specs=out_specs, check_vma=False
    )
```

time: 241 us -> 79.7 us (0.33)
  waiting for transfers between devices: 144 us -> 0 us
  Pallas kernels: 0 us -> 69 us
  blocking collectives: 35.8 us -> 0 us
  matrix products: 26 us -> 0 us
  between operations: 14.2 us -> 0.64 us
  starting transfers between devices: 12.8 us -> 0 us
  local copies, waits for them, and re-layouts: 2.72 us -> 8.71 us
  other arithmetic: 5.19 us -> 0 us
    pallas_call x0 -> x1, Pallas kernels: none -> 69 us  [on_device(): pl.pallas_call(kernel, out_shape=(jax.ShapeDtypeStruct(queries.shape, BF1...]
    reduce_scatter x1 -> x0, waiting for transfers between devices: 64.4 us -> none  [on_device(): lax.psum_scatter(down_terms.astype(jnp.bfloat16), 'mp', scatter_dimension...]
    all_gather x1 -> x0, waiting for transfers between devices: 58.8 us -> none  [on_device(): piece = lax.all_gather(slot_rows, 'mp', axis=1, tiled=True)]
    all_to_all x1 -> x0, blocking collectives: 35.8 us -> none  [on_device(): lax.all_to_all(outgoing, 'expert', split_axis=0, concat_axis=0, tiled=True)]
    dot_general x7 -> x0, matrix products: 26 us -> none  [the longest x1 8.19 us: on_device(): gate_sum = jnp.dot(piece, gate_matrix, preferred_element_type=jnp.float32)]
    all_to_all x2 -> x0, waiting for transfers between devices: 21 us -> none  [the longest x1 20.4 us: on_device(): lax.all_to_all(result.astype(jnp.bfloat16), 'expert', split_axis=0, conca...]
    all_to_all x2 -> x0, starting transfers between devices: 12.7 us -> none  [the longest x1 9.5 us: on_device(): lax.all_to_all(result.astype(jnp.bfloat16), 'expert', split_axis=0, conca...]
    unnamed x17 -> x4, local copies, waits for them, and re-layouts: 0.8 us -> 5.85 us
  transfers between devices with their start and end apart: 4 -> 0, of which waited for: 4 -> 0; matrix products, arithmetic and copies ran while one was open for 3% -> 0% of each run, Pallas kernels for 0% -> 0%
where the time goes in v1:
time: 79.7 us; the launch traced here: 78.4 us
  Pallas kernels  69 us (87%)
  local copies, waits for them, and re-layouts  8.71 us (11%)
    pallas_call x1, Pallas kernels, on_device(): pl.pallas_call(kernel, out_shape=(jax.ShapeDtypeStruct(queries.shape, BF1...  69 us
    unnamed x4, local copies, waits for them, and re-layouts  5.85 us

profile of v1, /device:TPU:0, one launch (start us, length us, event | category | flops | bytes accessed | tf_op | source)
XLA Modules:
  0.0 78.4 jit_solution(7781235759339470957)
XLA Ops:
  0.6 1.3 %reshape.7.gain_ref = f32[1,1536]{1,0:T(1,128)} reshape(f32[1536]{0:T(1024)} %param.17) | data formatting | bytes 12288 | tf_op jit(solution)/shard_map/reshape | solution.py:523
  1.9 1.4 %copy.15.ids_ref = s32[32,2]{1,0:T(8,128)} copy(s32[32,2]{0,1:T(2,128)} %param.18) | data formatting | bytes 512 | tf_op args[6]
  3.3 1.4 %copy.16.wts_ref = f32[32,2]{1,0:T(8,128)} copy(f32[32,2]{0,1:T(2,128)} %param.19) | data formatting | bytes 512 | tf_op args[7]
  4.7 1.6 %copy.14.q_ref = bf16[32,12,128]{2,1,0:T(8,128)(2,1)} copy(bf16[32,12,128]{2,0,1:T(8,128)(2,1)} %param.12) | data formatting | bytes 196608 | tf_op args[0]
  6.2 69.0 %shard_map.131 = (bf16[32,12,128]{2,1,0:T(8,128)(2,1)}, bf16[32,1536]{1,0:T(8,128)(2,1)}) custom-call(s32[32]{0:T(128)} %lengths.1, s32[8]{0:T(128)} %capacity.1, bf16[32,12,128]{2,1,0:T(8,128)(2,1)} %copy.14.q_ref, bf16[32,1536]{1,0:T(8,128)(2,1)} %x_ref.1, f32[1,1536]{1,0:T(1,128)} %reshape.7.gain_ref, s32[32,2]{1,0:T(8,128)} %copy.15.ids_ref, ...), custom_call_target="tpu_custom_call" | custom-call | tf_op jit(solution)/shard_map/pallas_call | solution.py:462
  75.3 1.6 %copy.17 = bf16[32,12,128]{2,0,1:T(8,128)(2,1)} copy(bf16[32,12,128]{2,1,0:T(8,128)(2,1)} %get-tuple-element.2) | data formatting | bytes 196608 | tf_op jit(solution)/shard_map/pallas_call | solution.py:462
  76.9 1.5 %copy.19 = bf16[32,1536]{1,0:T(8,128)(2,1)} copy(bf16[32,1536]{1,0:T(8,128)(2,1)} %get-tuple-element.7) | data formatting | bytes 196608

commit v2 on v1

--- a/solution.py
+++ b/solution.py
@@ -17,7 +17,7 @@
 HID = 512
 ROWS = 512
 SEQS = 32
-STEP = (0, 1, 3, 2)
+STEP = (1, 2, 3, 0)
 
 
 def base(h, p):
@@ -46,6 +46,9 @@
     wd,
     xb,
     pk,
+    zb,
+    yb,
+    rz,
     acc_g,
     acc_u,
     hid,
@@ -60,6 +63,8 @@
     rt,
     nm,
     fin,
+    qf,
+    cf,
     w_sem,
     kv_sem,
     sq_s,
@@ -68,6 +73,8 @@
     rt_r,
     nm_s,
     nm_r,
+    s0_s,
+    s0_r,
     s1_s,
     s1_r,
     xf_s,
@@ -80,6 +87,8 @@
     xq_r,
     r2_s,
     r2_r,
+    r3_s,
+    r3_r,
     fin_s,
     fin_r,
 ):
@@ -128,18 +137,28 @@
         copy.start()
 
     barrier = pltpu.get_barrier_semaphore()
-    partners = [plane(dz, dy) for dz in range(4) for dy in range(4) if (dz, dy) != (0, 0)]
+    partners = [plane(d, 0) for d in range(1, 4)] + [plane(0, d) for d in range(1, 4)]
     partners += [mate, near, far, opp, (s, m_both)]
     for device in partners:
         pl.semaphore_signal(barrier, inc=1, device_id=device, device_id_type=MESH)
 
     lane = lax.broadcasted_iota(jnp.int32, (TOK, 128), 1)
+    across = lax.broadcasted_iota(jnp.int32, (TOK, TOK), 1)
+    down_ward = lax.broadcasted_iota(jnp.int32, (TOK, TOK), 0)
+
+    def column(row):
+        return jnp.sum(jnp.where(across == down_ward, row, 0.0), axis=1, keepdims=True)
+
     ids = ids_ref[...].astype(F32)
     wts = wts_ref[...]
     route = jnp.where(
         lane == 0,
-        ids[:, 0:1],
-        jnp.where(lane == 1, ids[:, 1:2], jnp.where(lane == 2, wts[:, 0:1], wts[:, 1:2])),
+        column(ids[0:1]),
+        jnp.where(
+            lane == 1,
+            column(ids[1:2]),
+            jnp.where(lane == 2, column(wts[0:1]), column(wts[1:2])),
+        ),
     )
     rt[0] = route
     x = x_ref[...].astype(F32)
@@ -151,21 +170,16 @@
         send(sq.at[0], sq.at[k], sq_s, sq_r.at[k], (s, mates[k]))
     send(rt.at[0], rt.at[1], rt_s, rt_r, opp)
 
-    col = lax.broadcasted_iota(jnp.int32, (TOK, 256), 1)
-    group = col // 64
-    dz_col = jnp.where(group == 3, 2, jnp.where(group == 2, 3, group))
-    e_col = ((z + dz_col) % 4) * 2 + ((y + (col // 16) % 4) % 4) // 2
-    j_col = col % 16
-    cap_col = jnp.zeros((TOK, 256), jnp.int32)
+    col = lax.broadcasted_iota(jnp.int32, (TOK, 128), 1)
+    e_col = ((z + (col // 32 + 1) % 4) % 4) * 2 + (col // SLOTS) % 2
+    j_col = col % SLOTS
+    cap_col = jnp.zeros((TOK, 128), jnp.int32)
     for e in range(EXPERTS):
         cap_col = jnp.where(e_col == e, capacity[e], cap_col)
     open_col = j_col < cap_col
     e_col_f = e_col.astype(F32)
     j_col_f = j_col.astype(F32)
-    tri = (
-        lax.broadcasted_iota(jnp.int32, (TOK, TOK), 1)
-        < lax.broadcasted_iota(jnp.int32, (TOK, TOK), 0)
-    ).astype(F32).astype(BF16)
+    tri = (across < down_ward).astype(F32).astype(BF16)
 
     def routing(route):
         first = route[:, 0:1] == e_col_f
@@ -181,7 +195,7 @@
     for k in range(1, 4):
         wait(sq.at[k], sq_r.at[k])
     total = (sq[0] + sq[1] + sq[2] + sq[3])[:, 0:1]
-    normed = (x * lax.rsqrt(total / D + 1e-05) * gain_ref[...]).astype(BF16)
+    normed = (x * lax.rsqrt(total / D + 1e-05) * gain_ref[...].reshape(1, FEAT)).astype(BF16)
     nm[0] = normed
     send(nm.at[0], nm.at[1], nm_s, nm_r, opp)
 
@@ -190,25 +204,33 @@
             take, features, (((0,), (0,)), ((), ())), preferred_element_type=F32
         ).astype(BF16)
         pk[h] = packed
-        xb[0, 0, base(h, 0) : base(h, 0) + SLOTS, :] = packed[0:SLOTS, :]
-        for p in range(4):
-            for dy in range(4):
-                if p == 0 and dy == 0:
-                    continue
-                at = base(h, p) + dy * SLOTS
-                send(
-                    pk.at[h, pl.ds(p * 64 + dy * SLOTS, SLOTS), :],
-                    xb.at[0, 0, pl.ds(at, SLOTS), :],
-                    s1_s.at[h],
-                    s1_r.at[h, p],
-                    plane(STEP[p], dy),
-                )
+        zb[h, 96:128, :] = packed[96:128, :]
+        for p in (0, 2, 1):
+            rows = pl.ds(p * 32, 32)
+            send(
+                pk.at[h, rows, :], zb.at[h, rows, :], s0_s.at[h], s0_r.at[h, p], plane(STEP[p], 0)
+            )
+
+    def spread(h, p):
+        if p != 3:
+            wait(zb.at[h, pl.ds(p * 32, 32), :], s0_r.at[h, p])
+        for dy in range(4):
+            half = ((y + dy) % 4) // 2
+            src = pl.ds(pl.multiple_of(p * 32 + half * SLOTS, SLOTS), SLOTS)
+            at = base(h, p) + dy * SLOTS
+            if dy == 0:
+                xb[0, 0, at : at + SLOTS, :] = zb[h, src, :]
+                continue
+            send(
+                zb.at[h, src, :],
+                xb.at[0, 0, pl.ds(at, SLOTS), :],
+                s1_s.at[h],
+                s1_r.at[h, p],
+                plane(0, dy),
+            )
 
     def wait_slots(h, p):
-        if p == 0:
-            wait(xb.at[0, 0, pl.ds(base(h, p) + SLOTS, 48), :], s1_r.at[h, p])
-        else:
-            wait(xb.at[0, 0, pl.ds(base(h, p), 64), :], s1_r.at[h, p])
+        wait(xb.at[0, 0, pl.ds(base(h, p) + SLOTS, 48), :], s1_r.at[h, p])
 
     def to_mate(kx, h, p):
         rows = pl.ds(base(h, p), 64)
@@ -243,7 +265,7 @@
 
     def attend(b):
         scores = lax.dot_general(
-            q_ref[b],
+            qf[pl.ds(b, 12, stride=SEQS), :].astype(BF16),
             kv[b].reshape(256, 128),
             (((1,), (1,)), ((), ())),
             preferred_element_type=F32,
@@ -255,9 +277,9 @@
         both = jnp.concatenate(
             [jnp.where(low_head, probs, 0.0), jnp.where(low_head, 0.0, probs)], axis=1
         ).astype(BF16)
-        ctx_ref[b] = jnp.dot(
+        cf[pl.ds(b, 12, stride=SEQS), :] = jnp.dot(
             both, vv[b].reshape(256, 128), preferred_element_type=F32
-        ).astype(BF16)
+        )
 
     def attention(first, count):
         def some(i, carry):
@@ -268,23 +290,35 @@
         lax.fori_loop(0, count // 8, some, 0)
 
     pack(0, take_own, normed)
+    spread(0, 3)
+    qf[...] = q_ref[...].astype(F32).reshape(12 * SEQS, 128)
     k_copy.wait()
     v_copy.wait()
     attention(0, 8)
     wait(rt.at[1], rt_r)
     take_opp, weight_opp = routing(rt[1])
-    forward_own(0)
     wait(nm.at[1], nm_r)
     pack(1, take_opp, nm[1])
+    spread(0, 0)
+    forward_own(3)
+    spread(1, 3)
+    attention(8, 8)
+    spread(0, 1)
+    forward_own(0)
+    attention(16, 8)
+    spread(1, 0)
+    spread(0, 2)
+    forward_side(3)
+    spread(1, 1)
     forward_own(1)
-    attention(8, 8)
+    forward_opp(3)
+    spread(1, 2)
+    attention(24, 8)
+    ctx_ref[...] = cf[...].reshape(12, SEQS, 128).astype(BF16)
+    forward_opp(0)
+    forward_side(0)
     forward_own(2)
-    forward_opp(0)
-    attention(16, 8)
-    forward_own(3)
     forward_opp(1)
-    forward_side(0)
-    attention(24, 8)
 
     def gate_up(k, half):
         kx, cc = k // 2, k % 2
@@ -305,32 +339,6 @@
     def weights(kind, k):
         copies[k * 3 + kind].wait()
 
-    weights(0, 0)
-    weights(1, 0)
-    gate_up(0, 0)
-    forward_opp(2)
-    forward_side(1)
-    weights(0, 1)
-    weights(1, 1)
-    wait(xb.at[0, 1, pl.ds(0, 256), :], dd_r.at[0, 0])
-    gate_up(1, 0)
-    forward_opp(3)
-    gate_up(0, 1)
-    weights(0, 2)
-    weights(1, 2)
-    gate_up(2, 0)
-    forward_side(2)
-    wait(xb.at[0, 1, pl.ds(256, 256), :], dd_r.at[0, 1])
-    gate_up(1, 1)
-    weights(0, 3)
-    weights(1, 3)
-    wait(xb.at[1, 1, pl.ds(0, 256), :], dd_r.at[1, 0])
-    gate_up(3, 0)
-    forward_side(3)
-    gate_up(2, 1)
-    wait(xb.at[1, 1, pl.ds(256, 256), :], dd_r.at[1, 1])
-    gate_up(3, 1)
-
     def down(k, half, n):
         return jnp.dot(
             hid[half * 256 : half * 256 + 256, :],
@@ -360,24 +368,38 @@
                 device,
             )
 
-    def home(h, p, src, first):
+    def back_y(h, p, src, first):
         for dy in range(4):
-            at = pl.ds(p * 64 + dy * SLOTS, SLOTS)
-            if p == 0 and dy == 0:
-                rb[h, 0:SLOTS, :] = src[first : first + SLOTS, :]
+            at = p * 64 + dy * SLOTS
+            if dy == 0:
+                yb[h, at : at + SLOTS, :] = src[first : first + SLOTS, :]
                 continue
             send(
                 src.at[pl.ds(first + dy * SLOTS, SLOTS), :],
-                rb.at[h, at, :],
+                yb.at[h, pl.ds(at, SLOTS), :],
                 r2_s.at[h],
                 r2_r.at[h, p],
-                plane(-STEP[p] + 4, -dy + 4),
+                plane(0, 4 - dy),
             )
 
+    def back_z(h, p):
+        wait(yb.at[h, pl.ds(p * 64 + SLOTS, 48), :], r2_r.at[h, p])
+        for half in range(2):
+            terms = jnp.zeros((SLOTS, FEAT), F32)
+            for row in (2 * half, 2 * half + 1):
+                at = p * 64 + ((row - y + 4) % 4) * SLOTS
+                terms = terms + yb[h, pl.ds(pl.multiple_of(at, SLOTS), SLOTS), :].astype(F32)
+            dst = rz if p != 3 else rb
+            at = p * 32 + half * SLOTS
+            dst[h, at : at + SLOTS, :] = terms.astype(BF16)
+        if p != 3:
+            rows = pl.ds(p * 32, 32)
+            send(
+                rz.at[h, rows, :], rb.at[h, rows, :], r3_s.at[h], r3_r.at[h], plane(4 - STEP[p], 0)
+            )
+
     def wait_home(h):
-        wait(rb.at[h, pl.ds(SLOTS, 48), :], r2_r.at[h, 0])
-        for p in range(1, 4):
-            wait(rb.at[h, pl.ds(p * 64, 64), :], r2_r.at[h, p])
+        wait(rb.at[h, pl.ds(0, 96), :], r3_r.at[h])
 
     def combine(h, weight):
         high = weight.astype(BF16)
@@ -388,40 +410,69 @@
         terms = jnp.dot(stacked, rb[h], preferred_element_type=F32)
         return terms[0:TOK] + terms[TOK : 2 * TOK] + terms[2 * TOK : 3 * TOK]
 
-    weights(2, 3)
-    down_for_mate(1, 1)
-    down_for_mate(1, 0)
-    weights(2, 2)
-    down_mine(1, 1, q1)
-    to_sides(3)
-    to_sides(2)
-    down_mine(1, 0, q1)
-    to_sides(1)
-    to_sides(0)
-    weights(2, 1)
-    down_for_mate(0, 1)
-    down_for_mate(0, 0)
-    weights(2, 0)
-    down_mine(0, 1, q0)
-    home(1, 3, q0, base(1, 3))
-    home(1, 2, q0, base(1, 2))
-    down_mine(0, 0, q0)
-    home(1, 1, q0, base(1, 1))
-    home(1, 0, q0, base(1, 0))
-
-    for p in (3, 2, 1, 0):
+    def from_sides(p):
         rows = slice(p * 64, p * 64 + 64)
         for h in range(2):
             wait(xr.at[h, pl.ds(p * 64, 64), :], xq_r.at[h, p])
         terms = q0[base(0, p) : base(0, p) + 64, :].astype(F32)
         terms = terms + xr[0, rows, :].astype(F32) + xr[1, rows, :].astype(F32)
         own[rows, :] = terms.astype(BF16)
-        home(0, p, own, p * 64)
-        if p == 1:
-            wait_home(1)
-            fin[0] = combine(1, weight_opp).astype(BF16)
-            send(fin.at[0], fin.at[1], fin_s, fin_r, opp)
-
+        back_y(0, p, own, p * 64)
+
+    def from_mate(kx, half):
+        wait(xb.at[kx, 1, pl.ds(half * 256, 256), :], dd_r.at[kx, half])
+
+    for k in range(4):
+        weights(0, k)
+        weights(1, k)
+    gate_up(0, 0)
+    forward_side(1)
+    from_mate(0, 0)
+    gate_up(1, 0)
+    gate_up(2, 0)
+    forward_opp(2)
+    from_mate(1, 0)
+    gate_up(3, 0)
+    for k in range(4):
+        weights(2, k)
+    down_for_mate(1, 0)
+    gate_up(0, 1)
+    from_mate(0, 1)
+    gate_up(1, 1)
+    down_mine(1, 0, q1)
+    to_sides(0)
+    to_sides(1)
+    forward_side(2)
+    down_for_mate(0, 0)
+    gate_up(2, 1)
+    down_mine(0, 0, q0)
+    back_y(1, 0, q0, base(1, 0))
+    back_y(1, 1, q0, base(1, 1))
+    from_mate(1, 1)
+    gate_up(3, 1)
+    down_for_mate(1, 1)
+    down_for_mate(0, 1)
+    down_mine(1, 1, q1)
+    to_sides(2)
+    to_sides(3)
+    down_mine(0, 1, q0)
+    back_y(1, 2, q0, base(1, 2))
+    back_y(1, 3, q0, base(1, 3))
+    back_z(1, 0)
+    from_sides(0)
+    back_z(1, 1)
+    from_sides(1)
+    back_z(0, 0)
+    back_z(1, 2)
+    back_z(1, 3)
+    from_sides(2)
+    back_z(0, 1)
+    wait_home(1)
+    fin[0] = combine(1, weight_opp).astype(BF16)
+    send(fin.at[0], fin.at[1], fin_s, fin_r, opp)
+    back_z(0, 2)
+    from_sides(3)
+    back_z(0, 3)
     wait_home(0)
     added = combine(0, weight_own)
     wait(fin.at[1], fin_r)
@@ -431,13 +482,15 @@
     wait(rt.at[0], rt_s)
     wait(nm.at[0], nm_s)
     for h in range(2):
-        wait(pk.at[h, pl.ds(SLOTS, 240), :], s1_s.at[h])
+        wait(pk.at[h, pl.ds(0, 96), :], s0_s.at[h])
+        wait(xb.at[0, 0, pl.ds(0, 192), :], s1_s.at[h])
         wait(xb.at[0, 0, pl.ds(0, 256), :], xf_s.at[h])
         wait(xb.at[h, 0], dd_s.at[h])
         for half in range(2):
             wait(ps.at[h, half], pr_s.at[h, half])
         wait(xr.at[h], xq_s.at[h])
-        wait(rb.at[h, pl.ds(SLOTS, 240), :], r2_s.at[h])
+        wait(yb.at[h, pl.ds(0, 192), :], r2_s.at[h])
+        wait(rb.at[h, pl.ds(0, 96), :], r3_s.at[h])
     wait(fin.at[0], fin_s)
 
 
@@ -459,10 +512,10 @@
     smem = pl.BlockSpec(memory_space=pltpu.SMEM)
     hbm = pl.BlockSpec(memory_space=pl.ANY)
     dma = pltpu.SemaphoreType.DMA
-    return pl.pallas_call(
+    context, layer_out = pl.pallas_call(
         kernel,
         out_shape=(
-            jax.ShapeDtypeStruct(queries.shape, BF16),
+            jax.ShapeDtypeStruct((12, SEQS, 128), BF16),
             jax.ShapeDtypeStruct(moe_input.shape, BF16),
         ),
         in_specs=[smem, smem, vmem, vmem, vmem, vmem, vmem, hbm, hbm, hbm, hbm, hbm],
@@ -474,7 +527,10 @@
             pltpu.VMEM((4, FEAT, HID), BF16),
             pltpu.VMEM((4, HID, FEAT), BF16),
             pltpu.VMEM((2, 2, ROWS, FEAT), BF16),
+            pltpu.VMEM((2, 128, FEAT), BF16),
+            pltpu.VMEM((2, 128, FEAT), BF16),
             pltpu.VMEM((2, 256, FEAT), BF16),
+            pltpu.VMEM((2, 128, FEAT), BF16),
             pltpu.VMEM((ROWS, HID), F32),
             pltpu.VMEM((ROWS, HID), F32),
             pltpu.VMEM((ROWS, HID), BF16),
@@ -484,11 +540,13 @@
             pltpu.VMEM((ROWS, FEAT), BF16),
             pltpu.VMEM((2, 256, FEAT), BF16),
             pltpu.VMEM((256, FEAT), BF16),
-            pltpu.VMEM((2, 256, FEAT), BF16),
+            pltpu.VMEM((2, 128, FEAT), BF16),
             pltpu.VMEM((4, TOK, 128), F32),
             pltpu.VMEM((2, TOK, 128), F32),
             pltpu.VMEM((2, TOK, FEAT), BF16),
             pltpu.VMEM((2, TOK, FEAT), BF16),
+            pltpu.VMEM((12 * SEQS, 128), F32),
+            pltpu.VMEM((12 * SEQS, 128), F32),
             dma((3, 4)),
             dma((2,)),
             dma,
@@ -502,6 +560,8 @@
             dma((2,)),
             dma((2, 4)),
             dma((2,)),
+            dma((2, 4)),
+            dma((2,)),
             dma((2, 2)),
             dma((2, 2)),
             dma((2, 2)),
@@ -509,6 +569,8 @@
             dma((2, 4)),
             dma((2,)),
             dma((2, 4)),
+            dma((2,)),
+            dma((2,)),
             dma,
             dma,
         ],
@@ -518,17 +580,18 @@
     )(
         lengths,
         capacity,
-        queries,
+        queries.transpose(1, 0, 2),
         moe_input,
-        norm_gain.reshape(1, FEAT),
-        expert_ids,
-        combine_weights,
+        norm_gain,
+        expert_ids.T,
+        combine_weights.T,
         k_cache,
         v_cache,
         w_gate,
         w_up,
         w_down,
     )
+    return context.transpose(1, 0, 2), layer_out
 
 
 def solution(mesh):

time: 79.7 us -> 73.4 us (0.921); the launches traced: 78.4 us -> 73.2 us
  local copies, waits for them, and re-layouts: 8.71 us -> 3.08 us
    unnamed x4 -> x2, local copies, waits for them, and re-layouts: 5.85 us -> 3.08 us
    pallas_call x1 -> x0, local copies, waits for them, and re-layouts: 1.57 us -> none  [on_device(): pl.pallas_call(kernel, out_shape=(jax.ShapeDtypeStruct(queries.shape, BF1...]
    reshape x1 -> x0, local copies, waits for them, and re-layouts: 1.29 us -> none  [on_device(): norm_gain.reshape(1, FEAT)]
where the time goes in v2:
time: 73.4 us; the launch traced here: 73.2 us
  Pallas kernels  69.5 us (95%)
  local copies, waits for them, and re-layouts  3.08 us (4%)
    pallas_call x1, Pallas kernels, on_device(): pl.pallas_call(kernel, out_shape=(jax.ShapeDtypeStruct((12, SEQS, 128), B...  69.5 us
    unnamed x2, local copies, waits for them, and re-layouts  3.08 us

profile of v2, /device:TPU:0, one launch (start us, length us, event | category | flops | bytes accessed | tf_op | source)
XLA Modules:
  0.0 73.2 jit_solution(7387828267396931690)
XLA Ops:
  0.6 69.5 %shard_map.131 = (bf16[12,32,128]{2,1,0:T(8,128)(2,1)}, bf16[32,1536]{1,0:T(8,128)(2,1)}) custom-call(s32[32]{0:T(128)} %lengths.1, s32[8]{0:T(128)} %capacity.1, bf16[12,32,128]{2,1,0:T(8,128)(2,1)} %bitcast.4, bf16[32,1536]{1,0:T(8,128)(2,1)} %x_ref.1, f32[1536]{0:T(1024)} %gain_ref.1, s32[2,32]{1,0:T(2,128)} %bitcast.6, f32[2,32]{1,0:T(2,128)} %bitcast.7, ...), custom_call_target="tpu_custom_call" | custom-call | tf_op jit(solution)/shard_map/pallas_call | solution.py:515
  70.1 1.5 %copy.16 = bf16[32,12,128]{2,0,1:T(8,128)(2,1)} copy(bf16[32,12,128]{2,0,1:T(8,128)(2,1)} %bitcast.5) | data formatting | bytes 196608
  71.7 1.5 %copy.17 = bf16[32,1536]{1,0:T(8,128)(2,1)} copy(bf16[32,1536]{1,0:T(8,128)(2,1)} %get-tuple-element.9) | data formatting | bytes 196608

commit v3 on v2

--- a/solution.py
+++ b/solution.py
@@ -123,6 +123,12 @@
     def wait(ref, sem):
         pltpu.make_async_copy(ref, ref, sem).wait()
 
+    barrier = pltpu.get_barrier_semaphore()
+    partners = [plane(d, 0) for d in range(1, 4)] + [plane(0, d) for d in range(1, 4)]
+    partners += [mate, near, far, opp, (s, m_both)]
+    for device in partners:
+        pl.semaphore_signal(barrier, inc=1, device_id=device, device_id_type=MESH)
+
     copies = []
     for k in range(4):
         rows = pl.ds(pl.multiple_of(mates[k] * FEAT, FEAT), FEAT)
@@ -135,12 +141,6 @@
     v_copy.start()
     for copy in copies:
         copy.start()
-
-    barrier = pltpu.get_barrier_semaphore()
-    partners = [plane(d, 0) for d in range(1, 4)] + [plane(0, d) for d in range(1, 4)]
-    partners += [mate, near, far, opp, (s, m_both)]
-    for device in partners:
-        pl.semaphore_signal(barrier, inc=1, device_id=device, device_id_type=MESH)
 
     lane = lax.broadcasted_iota(jnp.int32, (TOK, 128), 1)
     across = lax.broadcasted_iota(jnp.int32, (TOK, TOK), 1)
@@ -258,66 +258,61 @@
             wait(xb.at[1, 0, pl.ds(base(h, p), 64), :], xf_r.at[h, p])
             to_mate(1, h, p)
 
-    position = lax.broadcasted_iota(jnp.int32, (12, 256), 1)
-    head = lax.broadcasted_iota(jnp.int32, (12, 128), 0)
-    low_head = head < 6
-    position = position[:, 0:128]
-
-    def attend(b):
-        scores = lax.dot_general(
-            qf[pl.ds(b, 12, stride=SEQS), :].astype(BF16),
-            kv[b].reshape(256, 128),
-            (((1,), (1,)), ((), ())),
-            preferred_element_type=F32,
-        )
-        scores = jnp.where(low_head, scores[:, 0:128], scores[:, 128:256]) * 128 ** (-0.5)
-        scores = jnp.where(position < lengths[b], scores, -jnp.inf)
+    position = lax.broadcasted_iota(jnp.int32, (16, 128), 1)
+    low_head = lax.broadcasted_iota(jnp.int32, (16, 128), 0) < 6
+    nowhere = jnp.zeros((16, 128), BF16)
+
+    def attention(first, count):
+        scores = []
+        for b in range(first, first + count):
+            both = lax.dot_general(
+                qf[pl.ds(b, 16, stride=SEQS), :].astype(BF16),
+                kv[b].reshape(256, 128),
+                (((1,), (1,)), ((), ())),
+                preferred_element_type=F32,
+            )
+            both = jnp.where(low_head, both[:, 0:128], both[:, 128:256]) * 128 ** (-0.5)
+            scores.append(jnp.where(position < lengths[b], both, -jnp.inf))
+        scores = jnp.concatenate(scores, axis=0)
         expo = jnp.exp(scores - jnp.max(scores, axis=1, keepdims=True))
-        probs = expo / jnp.sum(expo, axis=1, keepdims=True)
-        both = jnp.concatenate(
-            [jnp.where(low_head, probs, 0.0), jnp.where(low_head, 0.0, probs)], axis=1
-        ).astype(BF16)
-        cf[pl.ds(b, 12, stride=SEQS), :] = jnp.dot(
-            both, vv[b].reshape(256, 128), preferred_element_type=F32
-        )
-
-    def attention(first, count):
-        def some(i, carry):
-            for u in range(8):
-                attend(first + i * 8 + u)
-            return carry
-
-        lax.fori_loop(0, count // 8, some, 0)
+        probs = (expo / jnp.sum(expo, axis=1, keepdims=True)).astype(BF16)
+        for u in range(count):
+            mine = probs[u * 16 : u * 16 + 16]
+            both = jnp.concatenate(
+                [jnp.where(low_head, mine, nowhere), jnp.where(low_head, nowhere, mine)], axis=1
+            )
+            found = jnp.dot(both, vv[first + u].reshape(256, 128), preferred_element_type=F32)
+            cf[pl.ds(first + u, 12, stride=SEQS), :] = found[0:12]
 
     pack(0, take_own, normed)
     spread(0, 3)
-    qf[...] = q_ref[...].astype(F32).reshape(12 * SEQS, 128)
+    qf[0 : 12 * SEQS, :] = q_ref[...].astype(F32).reshape(12 * SEQS, 128)
+    qf[12 * SEQS : 16 * SEQS, :] = jnp.zeros((4 * SEQS, 128), F32)
     k_copy.wait()
     v_copy.wait()
-    attention(0, 8)
+    attention(0, 4)
+    attention(4, 4)
     wait(rt.at[1], rt_r)
     take_opp, weight_opp = routing(rt[1])
     wait(nm.at[1], nm_r)
     pack(1, take_opp, nm[1])
     spread(0, 0)
     forward_own(3)
-    spread(1, 3)
-    attention(8, 8)
+    attention(8, 4)
     spread(0, 1)
+    spread(0, 2)
+    attention(12, 4)
     forward_own(0)
-    attention(16, 8)
     spread(1, 0)
-    spread(0, 2)
-    forward_side(3)
     spread(1, 1)
     forward_own(1)
-    forward_opp(3)
+    spread(1, 3)
     spread(1, 2)
-    attention(24, 8)
-    ctx_ref[...] = cf[...].reshape(12, SEQS, 128).astype(BF16)
+    forward_side(3)
+    forward_own(2)
+    attention(16, 4)
     forward_opp(0)
     forward_side(0)
-    forward_own(2)
     forward_opp(1)
 
     def gate_up(k, half):
@@ -426,52 +421,57 @@
         weights(0, k)
         weights(1, k)
     gate_up(0, 0)
-    forward_side(1)
     from_mate(0, 0)
     gate_up(1, 0)
+    forward_opp(3)
+    forward_side(1)
     gate_up(2, 0)
-    forward_opp(2)
     from_mate(1, 0)
     gate_up(3, 0)
+    forward_opp(2)
     for k in range(4):
         weights(2, k)
     down_for_mate(1, 0)
     gate_up(0, 1)
-    from_mate(0, 1)
-    gate_up(1, 1)
+    forward_side(2)
     down_mine(1, 0, q1)
     to_sides(0)
     to_sides(1)
-    forward_side(2)
+    from_mate(0, 1)
+    gate_up(1, 1)
     down_for_mate(0, 0)
     gate_up(2, 1)
+    from_mate(1, 1)
+    gate_up(3, 1)
+    down_for_mate(1, 1)
     down_mine(0, 0, q0)
     back_y(1, 0, q0, base(1, 0))
     back_y(1, 1, q0, base(1, 1))
-    from_mate(1, 1)
-    gate_up(3, 1)
-    down_for_mate(1, 1)
-    down_for_mate(0, 1)
     down_mine(1, 1, q1)
     to_sides(2)
     to_sides(3)
+    from_sides(0)
+    down_for_mate(0, 1)
+    attention(20, 4)
     down_mine(0, 1, q0)
     back_y(1, 2, q0, base(1, 2))
     back_y(1, 3, q0, base(1, 3))
     back_z(1, 0)
-    from_sides(0)
+    from_sides(1)
+    attention(24, 4)
     back_z(1, 1)
-    from_sides(1)
     back_z(0, 0)
+    attention(28, 4)
+    ctx_ref[...] = cf[...].reshape(12, SEQS, 128).astype(BF16)
+    from_sides(2)
     back_z(1, 2)
     back_z(1, 3)
-    from_sides(2)
     back_z(0, 1)
+    from_sides(3)
     wait_home(1)
     fin[0] = combine(1, weight_opp).astype(BF16)
     send(fin.at[0], fin.at[1], fin_s, fin_r, opp)
     back_z(0, 2)
-    from_sides(3)
     back_z(0, 3)
     wait_home(0)
     added = combine(0, weight_own)
@@ -492,6 +492,11 @@
         wait(yb.at[h, pl.ds(0, 192), :], r2_s.at[h])
         wait(rb.at[h, pl.ds(0, 96), :], r3_s.at[h])
     wait(fin.at[0], fin_s)
+
+
+def hand_on(context_in, layer_in, context_out, layer_out):
+    context_out[...] = context_in[...]
+    layer_out[...] = layer_in[...]
 
 
 def on_device(
@@ -545,7 +550,7 @@
             pltpu.VMEM((2, TOK, 128), F32),
             pltpu.VMEM((2, TOK, FEAT), BF16),
             pltpu.VMEM((2, TOK, FEAT), BF16),
-            pltpu.VMEM((12 * SEQS, 128), F32),
+            pltpu.VMEM((16 * SEQS, 128), F32),
             pltpu.VMEM((12 * SEQS, 128), F32),
             dma((3, 4)),
             dma((2,)),
@@ -591,6 +596,15 @@
         w_up,
         w_down,
     )
+    context, layer_out = pl.pallas_call(
+        hand_on,
+        out_shape=(
+            jax.ShapeDtypeStruct(context.shape, BF16),
+            jax.ShapeDtypeStruct(layer_out.shape, BF16),
+        ),
+        in_specs=[vmem, vmem],
+        out_specs=(vmem, vmem),
+    )(context, layer_out)
     return context.transpose(1, 0, 2), layer_out
 
 

time: 73.4 us -> 69.3 us (0.944)
  local copies, waits for them, and re-layouts: 3.08 us -> 0 us
  Pallas kernels: 69.5 us -> 67.8 us
    pallas_call x1, Pallas kernels: 69.5 us -> 66.2 us  [on_device(): pl.pallas_call(kernel, out_shape=(jax.ShapeDtypeStruct((12, SEQS, 128), B...]
    unnamed x2 -> x0, local copies, waits for them, and re-layouts: 3.08 us -> none
    pallas_call x0 -> x1, Pallas kernels: none -> 1.62 us  [on_device(): pl.pallas_call(hand_on, out_shape=(jax.ShapeDtypeStruct(context.shape, BF...]
where the time goes in v3:
time: 69.3 us; the launch traced here: 68.4 us
  Pallas kernels  67.8 us (98%)
    pallas_call x1, Pallas kernels, on_device(): pl.pallas_call(kernel, out_shape=(jax.ShapeDtypeStruct((12, SEQS, 128), B...  66.2 us
    pallas_call x1, Pallas kernels, on_device(): pl.pallas_call(hand_on, out_shape=(jax.ShapeDtypeStruct(context.shape, BF...  1.62 us

profile of v3, /device:TPU:0, one launch (start us, length us, event | category | flops | bytes accessed | tf_op | source)
XLA Modules:
  0.0 68.4 jit_solution(13793644164574342479)
XLA Ops:
  0.6 66.2 %shard_map.131 = (bf16[12,32,128]{2,1,0:T(8,128)(2,1)}, bf16[32,1536]{1,0:T(8,128)(2,1)}) custom-call(s32[32]{0:T(128)} %lengths.1, s32[8]{0:T(128)} %capacity.1, bf16[12,32,128]{2,1,0:T(8,128)(2,1)} %bitcast.4, bf16[32,1536]{1,0:T(8,128)(2,1)} %x_ref.1, f32[1536]{0:T(1024)} %gain_ref.1, s32[2,32]{1,0:T(2,128)} %bitcast.5, f32[2,32]{1,0:T(2,128)} %bitcast.6, ...), custom_call_target="tpu_custom_call" | custom-call | tf_op jit(solution)/shard_map/pallas_call | solution.py:520
  66.8 1.6 %shard_map.132 = (bf16[12,32,128]{2,1,0:T(8,128)(2,1)}, bf16[32,1536]{1,0:T(8,128)(2,1)}) custom-call(bf16[12,32,128]{2,1,0:T(8,128)(2,1)} %get-tuple-element.6.context_in, bf16[32,1536]{1,0:T(8,128)(2,1)} %get-tuple-element.7.layer_in), custom_call_target="tpu_custom_call" | custom-call | tf_op jit(solution)/shard_map/pallas_call | solution.py:599

commit v4 on v3

--- a/solution.py
+++ b/solution.py
@@ -21,7 +21,8 @@
 
 
 def base(h, p):
-    return (p // 2) * 256 + h * 128 + (p % 2) * 64
+    place = (p + 1) % 4
+    return (place // 2) * 256 + h * 128 + (place % 2) * 64
 
 
 def kernel(
@@ -59,9 +60,11 @@
     xr,
     own,
     rb,
+    rd,
     sq,
     rt,
-    nm,
+    raw,
+    rs,
     fin,
     qf,
     cf,
@@ -71,8 +74,10 @@
     sq_r,
     rt_s,
     rt_r,
-    nm_s,
-    nm_r,
+    raw_s,
+    raw_r,
+    rs_s,
+    rs_r,
     s0_s,
     s0_r,
     s1_s,
@@ -89,6 +94,8 @@
     r2_r,
     r3_s,
     r3_r,
+    rd_s,
+    rd_r,
     fin_s,
     fin_r,
 ):
@@ -124,7 +131,8 @@
         pltpu.make_async_copy(ref, ref, sem).wait()
 
     barrier = pltpu.get_barrier_semaphore()
-    partners = [plane(d, 0) for d in range(1, 4)] + [plane(0, d) for d in range(1, 4)]
+    partners = [plane(2, 0)]
+    partners += [plane(dz, dy) for dz in (0, 1, 3) for dy in range(4) if (dz, dy) != (0, 0)]
     partners += [mate, near, far, opp, (s, m_both)]
     for device in partners:
         pl.semaphore_signal(barrier, inc=1, device_id=device, device_id_type=MESH)
@@ -169,35 +177,40 @@
     for k in range(1, 4):
         send(sq.at[0], sq.at[k], sq_s, sq_r.at[k], (s, mates[k]))
     send(rt.at[0], rt.at[1], rt_s, rt_r, opp)
+    send(x_ref, raw, raw_s, raw_r, opp)
 
     col = lax.broadcasted_iota(jnp.int32, (TOK, 128), 1)
     e_col = ((z + (col // 32 + 1) % 4) % 4) * 2 + (col // SLOTS) % 2
-    j_col = col % SLOTS
-    cap_col = jnp.zeros((TOK, 128), jnp.int32)
-    for e in range(EXPERTS):
-        cap_col = jnp.where(e_col == e, capacity[e], cap_col)
-    open_col = j_col < cap_col
-    e_col_f = e_col.astype(F32)
-    j_col_f = j_col.astype(F32)
+    last = lax.broadcasted_iota(jnp.int32, (TOK, 64), 1)
+    e_last = ((z + STEP[2]) % 4) * 2 + ((y + last // SLOTS) % 4) // 2
+
     tri = (across < down_ward).astype(F32).astype(BF16)
 
-    def routing(route):
-        first = route[:, 0:1] == e_col_f
-        second = route[:, 1:2] == e_col_f
+    def routing(route, e_col, j_col):
+        cap_col = jnp.zeros(e_col.shape, jnp.int32)
+        for e in range(EXPERTS):
+            cap_col = jnp.where(e_col == e, capacity[e], cap_col)
+        e_col = e_col.astype(F32)
+        first = route[:, 0:1] == e_col
+        second = route[:, 1:2] == e_col
         member = first | second
         rank = jnp.dot(tri, member.astype(F32).astype(BF16), preferred_element_type=F32)
-        take = member & (rank == j_col_f) & open_col
+        take = member & (rank == j_col.astype(F32)) & (j_col < cap_col)
         weight = jnp.where(take, jnp.where(first, route[:, 2:3], route[:, 3:4]), 0.0)
         return take.astype(F32).astype(BF16), weight
 
-    take_own, weight_own = routing(route)
+    take_own, weight_own = routing(route, e_col, col % SLOTS)
 
     for k in range(1, 4):
         wait(sq.at[k], sq_r.at[k])
     total = (sq[0] + sq[1] + sq[2] + sq[3])[:, 0:1]
-    normed = (x * lax.rsqrt(total / D + 1e-05) * gain_ref[...].reshape(1, FEAT)).astype(BF16)
-    nm[0] = normed
-    send(nm.at[0], nm.at[1], nm_s, nm_r, opp)
+    scale = lax.rsqrt(total / D + 1e-05)
+    rs[0] = jnp.broadcast_to(scale, (TOK, 128))
+    send(rs.at[0], rs.at[1], rs_s, rs_r, opp)
+    gain = gain_ref[...].reshape(1, FEAT)
+
+    def normed(tokens, scale):
+        return (tokens.astype(F32) * scale * gain).astype(BF16)
 
     def pack(h, take, features):
         packed = lax.dot_general(
@@ -234,19 +247,22 @@
 
     def to_mate(kx, h, p):
         rows = pl.ds(base(h, p), 64)
-        send(xb.at[kx, 0, rows, :], xb.at[kx, 1, rows, :], dd_s.at[kx], dd_r.at[kx, p // 2], mate)
-
-    def forward_own(p):
-        wait_slots(0, p)
-        rows = pl.ds(base(0, p), 64)
+        send(xb.at[kx, 0, rows, :], xb.at[kx, 1, rows, :], dd_s.at[kx], dd_r.at[kx, (p + 1) % 4 // 2], mate)
+
+    def cross(p, skip, count):
+        rows = pl.ds(base(0, p) + skip, count)
         send(xb.at[0, 0, rows, :], xb.at[1, 0, rows, :], xf_s.at[0], xf_r.at[0, p], near)
         send(
             xb.at[0, 0, rows, :],
-            xb.at[1, 0, pl.ds(base(1, p), 64), :],
+            xb.at[1, 0, pl.ds(base(1, p) + skip, count), :],
             xf_s.at[1],
             xf_r.at[1, p],
             far,
         )
+
+    def forward_own(p):
+        wait_slots(0, p)
+        cross(p, SLOTS, 48)
         to_mate(0, 0, p)
 
     def forward_opp(p):
@@ -284,36 +300,42 @@
             found = jnp.dot(both, vv[first + u].reshape(256, 128), preferred_element_type=F32)
             cf[pl.ds(first + u, 12, stride=SEQS), :] = found[0:12]
 
-    pack(0, take_own, normed)
+    pack(0, take_own, normed(x, scale))
     spread(0, 3)
+    cross(3, 0, SLOTS)
     qf[0 : 12 * SEQS, :] = q_ref[...].astype(F32).reshape(12 * SEQS, 128)
     qf[12 * SEQS : 16 * SEQS, :] = jnp.zeros((4 * SEQS, 128), F32)
     k_copy.wait()
     v_copy.wait()
     attention(0, 4)
+    weight_last = routing(route, e_last, last % SLOTS)[1]
+    weight_rest = jnp.where(col // 32 == 2, 0.0, weight_own)
+    rb[0, 64:96, :] = jnp.zeros((32, FEAT), BF16)
+    wait(rt.at[1], rt_r)
+    take_opp, weight_opp = routing(rt[1], e_col, col % SLOTS)
     attention(4, 4)
-    wait(rt.at[1], rt_r)
-    take_opp, weight_opp = routing(rt[1])
-    wait(nm.at[1], nm_r)
-    pack(1, take_opp, nm[1])
+    wait(raw, raw_r)
+    wait(rs.at[1], rs_r)
+    pack(1, take_opp, normed(raw[...], rs[1][:, 0:1]))
     spread(0, 0)
+    cross(0, 0, SLOTS)
     forward_own(3)
     attention(8, 4)
+    spread(1, 3)
     spread(0, 1)
-    spread(0, 2)
+    cross(1, 0, SLOTS)
     attention(12, 4)
     forward_own(0)
     spread(1, 0)
+    spread(0, 2)
+    cross(2, 0, SLOTS)
     spread(1, 1)
+    spread(1, 2)
+    attention(16, 4)
     forward_own(1)
-    spread(1, 3)
-    spread(1, 2)
+    forward_opp(3)
     forward_side(3)
-    forward_own(2)
-    attention(16, 4)
     forward_opp(0)
-    forward_side(0)
-    forward_opp(1)
 
     def gate_up(k, half):
         kx, cc = k // 2, k % 2
@@ -393,16 +415,24 @@
                 rz.at[h, rows, :], rb.at[h, rows, :], r3_s.at[h], r3_r.at[h], plane(4 - STEP[p], 0)
             )
 
-    def wait_home(h):
-        wait(rb.at[h, pl.ds(0, 96), :], r3_r.at[h])
-
-    def combine(h, weight):
+    def direct(p, src, first):
+        for dy in range(4):
+            rows = pl.ds(dy * SLOTS, SLOTS)
+            send(
+                src.at[pl.ds(first + dy * SLOTS, SLOTS), :],
+                rd.at[rows, :],
+                rd_s,
+                rd_r,
+                plane(4 - STEP[p], 4 - dy),
+            )
+
+    def combine(src, weight):
         high = weight.astype(BF16)
         rest = weight - high.astype(F32)
         middle = rest.astype(BF16)
         low = (rest - middle.astype(F32)).astype(BF16)
         stacked = jnp.concatenate([high, middle, low], axis=0)
-        terms = jnp.dot(stacked, rb[h], preferred_element_type=F32)
+        terms = jnp.dot(stacked, src, preferred_element_type=F32)
         return terms[0:TOK] + terms[TOK : 2 * TOK] + terms[2 * TOK : 3 * TOK]
 
     def from_sides(p):
@@ -412,7 +442,10 @@
         terms = q0[base(0, p) : base(0, p) + 64, :].astype(F32)
         terms = terms + xr[0, rows, :].astype(F32) + xr[1, rows, :].astype(F32)
         own[rows, :] = terms.astype(BF16)
-        back_y(0, p, own, p * 64)
+        if p == 2:
+            direct(p, own, p * 64)
+        else:
+            back_y(0, p, own, p * 64)
 
     def from_mate(kx, half):
         wait(xb.at[kx, 1, pl.ds(half * 256, 256), :], dd_r.at[kx, half])
@@ -421,66 +454,71 @@
         weights(0, k)
         weights(1, k)
     gate_up(0, 0)
+    forward_side(0)
     from_mate(0, 0)
     gate_up(1, 0)
-    forward_opp(3)
-    forward_side(1)
+    forward_own(2)
     gate_up(2, 0)
     from_mate(1, 0)
     gate_up(3, 0)
-    forward_opp(2)
+    forward_opp(1)
     for k in range(4):
         weights(2, k)
     down_for_mate(1, 0)
+    down_for_mate(0, 0)
+    forward_opp(2)
     gate_up(0, 1)
-    forward_side(2)
+    forward_side(1)
     down_mine(1, 0, q1)
     to_sides(0)
-    to_sides(1)
+    to_sides(3)
+    down_mine(0, 0, q0)
+    back_y(1, 0, q0, base(1, 0))
+    back_y(1, 3, q0, base(1, 3))
     from_mate(0, 1)
+    forward_side(2)
     gate_up(1, 1)
-    down_for_mate(0, 0)
     gate_up(2, 1)
     from_mate(1, 1)
     gate_up(3, 1)
     down_for_mate(1, 1)
-    down_mine(0, 0, q0)
-    back_y(1, 0, q0, base(1, 0))
-    back_y(1, 1, q0, base(1, 1))
-    down_mine(1, 1, q1)
-    to_sides(2)
-    to_sides(3)
-    from_sides(0)
     down_for_mate(0, 1)
     attention(20, 4)
+    down_mine(1, 1, q1)
+    to_sides(1)
+    to_sides(2)
+    from_sides(0)
     down_mine(0, 1, q0)
+    back_y(1, 1, q0, base(1, 1))
     back_y(1, 2, q0, base(1, 2))
-    back_y(1, 3, q0, base(1, 3))
     back_z(1, 0)
+    back_z(1, 3)
+    from_sides(3)
+    attention(24, 4)
+    back_z(0, 0)
+    back_z(1, 1)
     from_sides(1)
-    attention(24, 4)
-    back_z(1, 1)
-    back_z(0, 0)
+    back_z(1, 2)
     attention(28, 4)
     ctx_ref[...] = cf[...].reshape(12, SEQS, 128).astype(BF16)
+    back_z(0, 1)
     from_sides(2)
-    back_z(1, 2)
-    back_z(1, 3)
-    back_z(0, 1)
-    from_sides(3)
-    wait_home(1)
-    fin[0] = combine(1, weight_opp).astype(BF16)
+    back_z(0, 3)
+    wait(rb.at[1, pl.ds(0, 96), :], r3_r.at[1])
+    fin[0] = combine(rb[1], weight_opp).astype(BF16)
     send(fin.at[0], fin.at[1], fin_s, fin_r, opp)
-    back_z(0, 2)
-    back_z(0, 3)
-    wait_home(0)
-    added = combine(0, weight_own)
+    wait(rb.at[0, pl.ds(0, 64), :], r3_r.at[0])
+    added = combine(rb[0], weight_rest)
     wait(fin.at[1], fin_r)
-    out_ref[...] = (x_ref[...].astype(F32) + (added + fin[1].astype(F32))).astype(BF16)
+    added = added + fin[1].astype(F32)
+    wait(rd, rd_r)
+    added = added + combine(rd[...], weight_last)
+    out_ref[...] = (x_ref[...].astype(F32) + added).astype(BF16)
 
     wait(sq.at[pl.ds(0, 3)], sq_s)
     wait(rt.at[0], rt_s)
-    wait(nm.at[0], nm_s)
+    wait(raw, raw_s)
+    wait(rs.at[0], rs_s)
     for h in range(2):
         wait(pk.at[h, pl.ds(0, 96), :], s0_s.at[h])
         wait(xb.at[0, 0, pl.ds(0, 192), :], s1_s.at[h])
@@ -489,8 +527,9 @@
         for half in range(2):
             wait(ps.at[h, half], pr_s.at[h, half])
         wait(xr.at[h], xq_s.at[h])
-        wait(yb.at[h, pl.ds(0, 192), :], r2_s.at[h])
-        wait(rb.at[h, pl.ds(0, 96), :], r3_s.at[h])
+        wait(yb.at[h, pl.ds(0, 144 + 48 * h), :], r2_s.at[h])
+        wait(rb.at[h, pl.ds(0, 64 + 32 * h), :], r3_s.at[h])
+    wait(rd, rd_s)
     wait(fin.at[0], fin_s)
 
 
@@ -546,9 +585,11 @@
             pltpu.VMEM((2, 256, FEAT), BF16),
             pltpu.VMEM((256, FEAT), BF16),
             pltpu.VMEM((2, 128, FEAT), BF16),
+            pltpu.VMEM((64, FEAT), BF16),
             pltpu.VMEM((4, TOK, 128), F32),
             pltpu.VMEM((2, TOK, 128), F32),
-            pltpu.VMEM((2, TOK, FEAT), BF16),
+            pltpu.VMEM((TOK, FEAT), BF16),
+            pltpu.VMEM((2, TOK, 128), F32),
             pltpu.VMEM((2, TOK, FEAT), BF16),
             pltpu.VMEM((16 * SEQS, 128), F32),
             pltpu.VMEM((12 * SEQS, 128), F32),
@@ -560,6 +601,8 @@
             dma,
             dma,
             dma,
+            dma,
+            dma,
             dma((2,)),
             dma((2, 4)),
             dma((2,)),
@@ -576,6 +619,8 @@
             dma((2, 4)),
             dma((2,)),
             dma((2,)),
+            dma,
+            dma,
             dma,
             dma,
         ],

time: 69.3 us -> 68 us (0.981)
  Pallas kernels: 67.8 us -> 66.8 us
    pallas_call x1, Pallas kernels: 66.2 us -> 65.1 us  [on_device(): pl.pallas_call(kernel, out_shape=(jax.ShapeDtypeStruct((12, SEQS, 128), B...]
where the time goes in v4:
time: 68 us; the launch traced here: 67.4 us
  Pallas kernels  66.8 us (98%)
    pallas_call x1, Pallas kernels, on_device(): pl.pallas_call(kernel, out_shape=(jax.ShapeDtypeStruct((12, SEQS, 128), B...  65.1 us
    pallas_call x1, Pallas kernels, on_device(): pl.pallas_call(hand_on, out_shape=(jax.ShapeDtypeStruct(context.shape, BF...  1.62 us

profile of v4, /device:TPU:0, one launch (start us, length us, event | category | flops | bytes accessed | tf_op | source)
XLA Modules:
  0.0 67.4 jit_solution(13390817147185421240)
XLA Ops:
  0.6 65.1 %shard_map.131 = (bf16[12,32,128]{2,1,0:T(8,128)(2,1)}, bf16[32,1536]{1,0:T(8,128)(2,1)}) custom-call(s32[32]{0:T(128)} %lengths.1, s32[8]{0:T(128)} %capacity.1, bf16[12,32,128]{2,1,0:T(8,128)(2,1)} %bitcast.4, bf16[32,1536]{1,0:T(8,128)(2,1)} %x_ref.1, f32[1536]{0:T(1024)} %gain_ref.1, s32[2,32]{1,0:T(2,128)} %bitcast.5, f32[2,32]{1,0:T(2,128)} %bitcast.6, ...), custom_call_target="tpu_custom_call" | custom-call | tf_op jit(solution)/shard_map/pallas_call | solution.py:559
  65.8 1.6 %shard_map.132 = (bf16[12,32,128]{2,1,0:T(8,128)(2,1)}, bf16[32,1536]{1,0:T(8,128)(2,1)}) custom-call(bf16[12,32,128]{2,1,0:T(8,128)(2,1)} %get-tuple-element.6.context_in, bf16[32,1536]{1,0:T(8,128)(2,1)} %get-tuple-element.7.layer_in), custom_call_target="tpu_custom_call" | custom-call | tf_op jit(solution)/shard_map/pallas_call | solution.py:644

commit v5 on v4

--- a/solution.py
+++ b/solution.py
@@ -495,10 +495,10 @@
     back_z(1, 3)
     from_sides(3)
     attention(24, 4)
+    back_z(1, 1)
     back_z(0, 0)
-    back_z(1, 1)
+    back_z(1, 2)
     from_sides(1)
-    back_z(1, 2)
     attention(28, 4)
     ctx_ref[...] = cf[...].reshape(12, SEQS, 128).astype(BF16)
     back_z(0, 1)

time: 68 us -> 67.5 us (level)
  no operation moved by 1% of the time
where the time goes in v5:
time: 67.5 us; the launch traced here: 67.1 us
  Pallas kernels  66.5 us (99%)
    pallas_call x1, Pallas kernels, on_device(): pl.pallas_call(kernel, out_shape=(jax.ShapeDtypeStruct((12, SEQS, 128), B...  64.9 us
    pallas_call x1, Pallas kernels, on_device(): pl.pallas_call(hand_on, out_shape=(jax.ShapeDtypeStruct(context.shape, BF...  1.62 us

profile of v5, /device:TPU:0, one launch (start us, length us, event | category | flops | bytes accessed | tf_op | source)
XLA Modules:
  0.0 67.1 jit_solution(5354768330305629825)
XLA Ops:
  0.6 64.9 %shard_map.131 = (bf16[12,32,128]{2,1,0:T(8,128)(2,1)}, bf16[32,1536]{1,0:T(8,128)(2,1)}) custom-call(s32[32]{0:T(128)} %lengths.1, s32[8]{0:T(128)} %capacity.1, bf16[12,32,128]{2,1,0:T(8,128)(2,1)} %bitcast.4, bf16[32,1536]{1,0:T(8,128)(2,1)} %x_ref.1, f32[1536]{0:T(1024)} %gain_ref.1, s32[2,32]{1,0:T(2,128)} %bitcast.5, f32[2,32]{1,0:T(2,128)} %bitcast.6, ...), custom_call_target="tpu_custom_call" | custom-call | tf_op jit(solution)/shard_map/pallas_call | solution.py:559
  65.5 1.6 %shard_map.132 = (bf16[12,32,128]{2,1,0:T(8,128)(2,1)}, bf16[32,1536]{1,0:T(8,128)(2,1)}) custom-call(bf16[12,32,128]{2,1,0:T(8,128)(2,1)} %get-tuple-element.6.context_in, bf16[32,1536]{1,0:T(8,128)(2,1)} %get-tuple-element.7.layer_in), custom_call_target="tpu_custom_call" | custom-call | tf_op jit(solution)/shard_map/pallas_call | solution.py:644
